TPU v7x, 32 devices: a whole 2x2x4 slice. The times are simulated.
32 devices in a mesh: row: 8 (over z, core), col: 4 (over y, x).
Axes of the slice: x: 2, y: 2, z: 4, core: 2. Of those that a mesh axis runs over, the one named last changes fastest.
Arguments:
- pair_exchange: bfloat16 [64, 16, 1024], P(('row', 'col')), may hold values from -6 to 6
- conduction: bfloat16 [64, 4, 1024], P(('row', 'col')), may hold values from -6 to 6
- valence: bfloat16 [64, 4, 1024], P(('row', 'col')), may hold values from -6 to 6
- coulomb: float32 [1024], replicated, may hold values from 0.5 to 5
- screening: float32 [34, 1024], replicated, may hold values from 0.1 to 1
- energies: float32 [64, 16], P(('row', 'col')), may hold values from 1 to 9
- vectors: bfloat16 [64, 512], P(('row', 'col')), may hold values from -6 to 6
- k_coords: int32 [64, 2], P(('row', 'col')), may hold values from 0 to 31, as said below
Outputs:
- residual_block: float32 [64, 512], P(('row', 'col'))
- alpha: float32 [32, 32], replicated
Inputs may be any that keep to these rules, and one draw needn't show every extreme that they name: `k_coords`: each row holds a k-point's coordinates on the periodic 32 x 2 mesh, first then second; every mesh point occurs exactly once.
All inputs are finite; a program needn't handle non-finite values.
Results may differ from a plain program's by a relative error of at most 0.0028.
Values may be sent and summed in bfloat16 or wider, within the bound.
A program may use at most 64 MiB of HBM per device.

v0:
```python
import jax
import jax.numpy as jnp
from jax import lax
from jax.sharding import PartitionSpec as P

MX = 32
highest = lax.Precision.HIGHEST


def pair_factors(conduction, valence):
    count, valence_count, plane_count = valence.shape
    joined = (
        valence.astype(jnp.float32)[:, :, None, :] * conduction.astype(jnp.float32)[:, None, :, :]
    )
    return joined.reshape(count, valence_count * conduction.shape[1], plane_count).astype(
        jnp.bfloat16
    )


def transfer_index(rows_at, cols_at, mesh_cols):
    delta_first = jnp.mod(rows_at[:, None, 0] - cols_at[None, :, 0], MX)
    delta_second = jnp.mod(rows_at[:, None, 1] - cols_at[None, :, 1], mesh_cols)
    fold_first = jnp.minimum(delta_first, MX - delta_first)
    fold_second = jnp.minimum(delta_second, mesh_cols - delta_second)
    return (fold_first * (mesh_cols // 2 + 1) + fold_second).astype(jnp.int32)


def on_device(pair_exchange, conduction, valence, coulomb, screening, energies, vectors, k_coords):
    local_count, band_count, plane_count = pair_exchange.shape
    vector_count = vectors.shape[1] // band_count
    row_count = lax.axis_size("row")
    col_count = lax.axis_size("col")
    total_count = local_count * row_count * col_count
    mesh_cols = total_count // MX
    moving = vectors.reshape(local_count, band_count, vector_count)
    partial_density = jnp.einsum(
        "ktg,ktn->gn", pair_exchange, moving, preferred_element_type=jnp.float32
    )
    density = lax.psum(partial_density, ("row", "col"))
    block_size = 128
    sweeps = plane_count // block_size
    col_cond, col_val, col_vec, col_at = (
        lax.all_gather(conduction, "row", axis=0, tiled=True),
        lax.all_gather(valence, "row", axis=0, tiled=True),
        lax.all_gather(vectors, "row", axis=0, tiled=True),
        lax.all_gather(k_coords, "row", axis=0, tiled=True),
    )
    row_cond, row_val, row_at = (
        lax.all_gather(conduction, "col", axis=0, tiled=True),
        lax.all_gather(valence, "col", axis=0, tiled=True),
        lax.all_gather(k_coords, "col", axis=0, tiled=True),
    )
    row_pairs = pair_factors(row_cond, row_val)
    col_pairs = pair_factors(col_cond, col_val)
    indices = transfer_index(row_at, col_at, mesh_cols)
    col_moving = col_vec.reshape(-1, band_count, vector_count)

    def square_sweep(sweep_index, running):
        anchor = sweep_index * block_size
        coupling = jnp.take(
            lax.dynamic_slice_in_dim(screening, anchor, block_size, 1), indices, axis=0
        )
        row_block = lax.dynamic_slice_in_dim(row_pairs, anchor, block_size, 2)
        col_block = lax.dynamic_slice_in_dim(col_pairs, anchor, block_size, 2)
        col_proj = jnp.einsum(
            "ktg,ktn->kng", col_block, col_moving, preferred_element_type=jnp.float32
        )
        potential = jnp.einsum("ijg,jng->ing", coupling, col_proj, precision=highest)
        return running + jnp.einsum(
            "ktg,kng->ktn", row_block.astype(jnp.float32), potential, precision=highest
        )

    forward = lax.fori_loop(
        0,
        sweeps,
        square_sweep,
        jnp.zeros((row_pairs.shape[0], band_count, vector_count), jnp.float32),
    )
    owned = lax.psum_scatter(
        forward.reshape(col_count, local_count, band_count, vector_count),
        "col",
        scatter_dimension=0,
        tiled=True,
    )[0]
    moving_wide = moving.astype(jnp.float32)
    exchange_term = jnp.einsum(
        "ktg,gn->ktn", pair_exchange.astype(jnp.float32) * coulomb, density, precision=highest
    )
    applied = (
        energies[:, :, None] * moving_wide
        + 2.0 / (total_count * band_count) * exchange_term
        - owned / total_count
    )
    gram = jnp.einsum("ktm,ktn->mn", moving_wide, applied, precision=highest)
    alpha = lax.psum(gram, ("row", "col")) / (total_count * band_count)
    residual = applied - jnp.einsum("ktm,mn->ktn", moving_wide, alpha, precision=highest)
    return (residual.reshape(local_count, band_count * vector_count), alpha)


def solution(mesh):
    in_specs = (
        P(("row", "col"), None, None),
        P(("row", "col"), None, None),
        P(("row", "col"), None, None),
        P(),
        P(),
        P(("row", "col"), None),
        P(("row", "col"), None),
        P(("row", "col"), None),
    )
    out_specs = (P(("row", "col"), None), P())
    return jax.shard_map(
        on_device, mesh=mesh, in_specs=in_specs, out_specs=out_specs, check_vma=False
    )
```

profile of v0, /device:TPU:0, one launch (start us, length us, event | category | flops | bytes accessed | tf_op | source)
XLA Modules:
  0.0 299.9 jit_solution(13418184121838847277)
XLA Ops:
  8.1 0.6 copy-done.6
  8.7 13.5 %all-gather.2 = s32[8,2,2]{2,1,0:T(2,128)S(1)} all-gather(s32[1,2,2]{2,1,0:T(2,128)S(1)} %bitcast.65), channel_id=1, replica_groups=mesh['row'=8,'col'=4] {'row'}, dimensions={0}, use_global_device_ids=true | all-gather | bytes 144 | tf_op jit(solution)/shard_map/all_gather | solution.py:46
  22.1 8.1 %all-gather.1 = s32[4,2,2]{2,1,0:T(2,128)S(1)} all-gather(s32[1,2,2]{2,1,0:T(2,128)S(1)} %bitcast.66), channel_id=1, replica_groups=mesh['row'=8,'col'=4] {'col'}, dimensions={0}, use_global_device_ids=true | all-gather | bytes 80 | tf_op jit(solution)/shard_map/all_gather | solution.py:51
  30.2 14.3 %all_gather.23 = bf16[16,4,1024]{2,1,0:T(4,128)(2,1)S(1)} all-gather(bf16[2,4,1024]{2,1,0:T(4,128)(2,1)} %param.12), channel_id=1, replica_groups=mesh['row'=8,'col'=4] {'row'}, dimensions={0}, use_global_device_ids=true | all-gather | bytes 147456 | tf_op jit(solution)/shard_map/all_gather | solution.py:44
  44.5 8.3 %all_gather.21 = bf16[8,4,1024]{2,1,0:T(4,128)(2,1)S(1)} all-gather(bf16[2,4,1024]{2,1,0:T(4,128)(2,1)S(1)} %copy-done.2), channel_id=1, replica_groups=mesh['row'=8,'col'=4] {'col'}, dimensions={0}, use_global_device_ids=true | all-gather | bytes 81920 | tf_op jit(solution)/shard_map/all_gather | solution.py:50
  52.9 14.0 %all_gather.24 = bf16[16,4,1024]{2,1,0:T(4,128)(2,1)S(1)} all-gather(bf16[2,4,1024]{2,1,0:T(4,128)(2,1)S(1)} %copy-done.3), channel_id=1, replica_groups=mesh['row'=8,'col'=4] {'row'}, dimensions={0}, use_global_device_ids=true | all-gather | bytes 147456 | tf_op jit(solution)/shard_map/all_gather | solution.py:43
  66.9 7.2 %all_gather.22 = bf16[8,4,1024]{2,1,0:T(4,128)(2,1)S(1)} all-gather(bf16[2,4,1024]{2,1,0:T(4,128)(2,1)S(1)} %copy-done.3), channel_id=1, replica_groups=mesh['row'=8,'col'=4] {'col'}, dimensions={0}, use_global_device_ids=true | all-gather | bytes 81920 | tf_op jit(solution)/shard_map/all_gather | solution.py:49
  75.2 0.6 copy-done.4
  75.8 12.8 %all-gather = bf16[8,2,512]{2,1,0:T(2,128)(2,1)S(1)} all-gather(bf16[1,2,512]{2,1,0:T(2,128)(2,1)S(1)} %bitcast.64), channel_id=1, replica_groups=mesh['row'=8,'col'=4] {'row'}, dimensions={0}, use_global_device_ids=true | all-gather | bytes 18432 | tf_op jit(solution)/shard_map/all_gather | solution.py:45
  88.7 33.2 %while.14 = (s32[]{:T(128)}, f32[8,16,32]{2,1,0:T(8,128)S(1)}, bf16[8,16,1024]{2,1,0:T(8,128)(2,1)S(1)}, bf16[16,16,1024]{2,1,0:T(8,128)(2,1)S(1)}, bf16[16,16,3...) while((s32[]{:T(128)}, f32[8,16,32]{2,1,0:T(8,128)S(1)}, ...), condition=%wide.region_2.3_spmd.clone, body=%wide.region_1.2_spmd.clone.sunk | while | flops 14714503 | bytes 2319689 | solution.py:73
  88.7 0.7 constant_dynamic-slice_fusion.2
  89.6 0.6 gather_fusion
  90.8 0.5 copy.39
  91.4 1.1 convolution_bitcast_fusion.8
  92.9 0.7 constant_dynamic-slice_fusion.2
  93.8 0.6 gather_fusion
  94.9 0.5 copy.39
  95.5 1.1 convolution_bitcast_fusion.8
  97.0 0.7 constant_dynamic-slice_fusion.2
  97.9 0.6 gather_fusion
  99.1 0.5 copy.39
  99.7 1.1 convolution_bitcast_fusion.8
  101.2 0.7 constant_dynamic-slice_fusion.2
  102.1 0.6 gather_fusion
  103.2 0.5 copy.39
  103.8 1.1 convolution_bitcast_fusion.8
  105.3 0.7 constant_dynamic-slice_fusion.2
  106.2 0.6 gather_fusion
  107.4 0.5 copy.39
  108.0 1.1 convolution_bitcast_fusion.8
  109.5 0.7 constant_dynamic-slice_fusion.2
  110.4 0.6 gather_fusion
  111.5 0.5 copy.39
  112.1 1.1 convolution_bitcast_fusion.8
  113.6 0.7 constant_dynamic-slice_fusion.2
  114.5 0.6 gather_fusion
  116.3 1.1 convolution_bitcast_fusion.8
  117.8 0.7 constant_dynamic-slice_fusion.2
  118.7 0.6 gather_fusion
  120.4 1.1 convolution_bitcast_fusion.8
  121.9 0.6 copy-done
  122.8 0.9 convolution_bitcast_fusion.2
  123.7 20.8 %reduce-scatter.4.cloned.1.call-done = f32[1,2,16,32]{3,2,1,0:T(8,128)} async-done(((f32[4,2,16,32]{3,2,1,0:T(8,128)}), f32[1,2,16,32]{3,2,1,0:T(8,128)}) %reduce-scatter.4.cloned.1.call-update) | async-done | bytes 4112
  144.5 105.8 %all-reduce.3.cloned.1.call-done = f32[1024,32]{0,1:T(8,128)} async-done(((f32[1024,32]{0,1:T(8,128)}), f32[1024,32]{0,1:T(8,128)}) %all-reduce.3.cloned.1.call-update) | async-done | bytes 131088 | tf_op jit(solution)/shard_map/psum | solution.py:39
  250.3 1.1 fusion.17
  251.7 39.3 %psum.15 = f32[32,32]{0,1:T(8,128)S(1)} all-reduce(f32[32,32]{0,1:T(8,128)S(1)} %convolution_bitcast_fusion.4), channel_id=1, replica_groups=mesh['row'=8,'col'=4] {'row','col'}, use_global_device_ids=true, to_apply=%region_4.5 | all-reduce | flops 1024 | bytes 8192 | tf_op jit(solution)/shard_map/psum | solution.py:95
  291.1 0.7 reshape.61
  291.8 0.7 copy.24
  (95 shorter events, 11.9 us)
Async XLA Ops:
  8.0 0.7 copy-start.6
  8.0 136.5 %reduce-scatter.4.cloned.1.call-start = ((), (), s32[]{:S(2)}) async-start(), calls=%async_computation.2 | async-start | bytes 81920
  30.2 14.3 %copy-start.2 = (bf16[2,4,1024]{2,1,0:T(4,128)(2,1)S(1)}, bf16[2,4,1024]{2,1,0:T(4,128)(2,1)}, u32[]{:S(2)}) copy-start(bf16[2,4,1024]{2,1,0:T(4,128)(2,1)} %param.12) | copy-start | bytes 49156
  44.5 8.3 %copy-start.3 = (bf16[2,4,1024]{2,1,0:T(4,128)(2,1)S(1)}, bf16[2,4,1024]{2,1,0:T(4,128)(2,1)}, u32[]{:S(2)}) copy-start(bf16[2,4,1024]{2,1,0:T(4,128)(2,1)} %param.11) | copy-start | bytes 49156
  75.2 0.7 copy-start.4
  121.9 0.6 copy-start
  121.9 0.9 copy-start.1
  122.6 127.7 %all-reduce.3.cloned.1.call-start = ((), (), s32[]{:S(2)}) async-start(), calls=%async_computation.1 | async-start | bytes 262144 | tf_op jit(solution)/shard_map/psum | solution.py:39
  123.7 126.6 %copy-start.5 = (f32[1024]{0:T(1024)S(1)}, f32[1024]{0:T(1024)}, u32[]{:S(2)}) copy-start(f32[1024]{0:T(1024)} %param.13) | copy-start | bytes 12292
  123.7 126.7 %copy-start.7 = (f32[2,16]{1,0:T(2,128)S(1)}, f32[2,16]{1,0:T(2,128)}, u32[]{:S(2)}) copy-start(f32[2,16]{1,0:T(2,128)} %param.15) | copy-start | bytes 388
Sparse Core Ops, SparseCore 0:
  122.7 21.7 reduce-scatter.3
Sparse Core Ops, SparseCore 1:
  128.6 121.7 all-reduce.2
where the time goes:
time: 301 us; the launch traced here: 300 us
  waiting for transfers between devices  127 us (42%)
  blocking collectives  117 us (39%)
  local copies, waits for them, and re-layouts  21.7 us (7%)
  matrix products  16.1 us (5%)
  between operations  15.6 us (5%)
    psum x1, waiting for transfers between devices, on_device(): density = lax.psum(partial_density, ('row', 'col'))  106 us
    psum x1, blocking collectives, on_device(): alpha = lax.psum(gram, ('row', 'col')) / (total_count * band_count)  39.3 us
    unnamed x3, waiting for transfers between devices  20.8 us
    all_gather x1, blocking collectives, on_device(): lax.all_gather(valence, 'row', axis=0, tiled=True)  14.3 us
    all_gather x1, blocking collectives, on_device(): lax.all_gather(conduction, 'row', axis=0, tiled=True)  14 us
    all_gather x1, blocking collectives, on_device(): lax.all_gather(k_coords, 'row', axis=0, tiled=True)  13.5 us
    all_gather x1, blocking collectives, on_device(): lax.all_gather(vectors, 'row', axis=0, tiled=True)  12.8 us
    dot_general x8, matrix products, square_sweep(): jnp.einsum('ijg,jng->ing', coupling, col_proj, precision=highest)  8.7 us
  transfers between devices with their start and end apart: 2, of which 2 were waited for; matrix products, arithmetic and copies ran while one was open for 0% of the time, Pallas kernels for 0%

commit v1 on v0

--- a/solution.py
+++ b/solution.py
@@ -36,7 +36,8 @@
     partial_density = jnp.einsum(
         "ktg,ktn->gn", pair_exchange, moving, preferred_element_type=jnp.float32
     )
-    density = lax.psum(partial_density, ("row", "col"))
+    one_axis = lax.psum(partial_density, "row")
+    density = lax.psum(one_axis, "col")
     block_size = 128
     sweeps = plane_count // block_size
     col_cond, col_val, col_vec, col_at = (

time: 301 us -> 242 us (0.80)
  waiting for transfers between devices: 127 us -> 66.3 us
    psum x1 -> x2, waiting for transfers between devices: 106 us -> 44.5 us  [the longest x1 44.5 us: on_device(): density = lax.psum(one_axis, 'col')]
    unnamed x3 -> x4, waiting for transfers between devices: 20.8 us -> 21.7 us
  transfers between devices with their start and end apart: 2 -> 3, of which waited for: 2 -> 2; matrix products, arithmetic and copies ran while one was open for 0% -> 14% of each run, Pallas kernels for 0% -> 0%
where the time goes in v1:
time: 242 us; the launch traced here: 241 us
  blocking collectives  117 us (48%)
  waiting for transfers between devices  66.3 us (27%)
  local copies, waits for them, and re-layouts  22.3 us (9%)
  matrix products  17 us (7%)
  between operations  15.6 us (6%)
    psum x1, waiting for transfers between devices, on_device(): density = lax.psum(one_axis, 'col')  44.5 us
    psum x1, blocking collectives, on_device(): alpha = lax.psum(gram, ('row', 'col')) / (total_count * band_count)  39.3 us
    unnamed x4, waiting for transfers between devices  21.7 us
    all_gather x1, blocking collectives, on_device(): lax.all_gather(conduction, 'row', axis=0, tiled=True)  14 us
    all_gather x1, blocking collectives, on_device(): lax.all_gather(valence, 'row', axis=0, tiled=True)  13.9 us
    all_gather x1, blocking collectives, on_device(): lax.all_gather(k_coords, 'row', axis=0, tiled=True)  13.5 us
    all_gather x1, blocking collectives, on_device(): lax.all_gather(vectors, 'row', axis=0, tiled=True)  12.8 us
    dot_general x8, matrix products, square_sweep(): jnp.einsum('ijg,jng->ing', coupling, col_proj, precision=highest)  8.74 us
  transfers between devices with their start and end apart: 3, of which 2 were waited for; matrix products, arithmetic and copies ran while one was open for 14% of the time, Pallas kernels for 0%

profile of v1, /device:TPU:0, one launch (start us, length us, event | category | flops | bytes accessed | tf_op | source)
XLA Modules:
  0.0 240.8 jit_solution(13974464845383612156)
XLA Ops:
  8.0 0.8 reshape.58
  8.8 1.7 convolution_bitcast_fusion.2
  10.6 0.6 copy-done.6
  11.2 13.5 %all-gather.2 = s32[8,2,2]{2,1,0:T(2,128)S(1)} all-gather(s32[1,2,2]{2,1,0:T(2,128)S(1)} %bitcast.65), channel_id=1, replica_groups=mesh['row'=8,'col'=4] {'row'}, dimensions={0}, use_global_device_ids=true | all-gather | bytes 144 | tf_op jit(solution)/shard_map/all_gather | solution.py:47
  24.7 8.1 %all-gather.1 = s32[4,2,2]{2,1,0:T(2,128)S(1)} all-gather(s32[1,2,2]{2,1,0:T(2,128)S(1)} %bitcast.66), channel_id=1, replica_groups=mesh['row'=8,'col'=4] {'col'}, dimensions={0}, use_global_device_ids=true | all-gather | bytes 80 | tf_op jit(solution)/shard_map/all_gather | solution.py:52
  32.8 13.9 %all_gather.23 = bf16[16,4,1024]{2,1,0:T(4,128)(2,1)S(1)} all-gather(bf16[2,4,1024]{2,1,0:T(4,128)(2,1)S(1)} %copy-done.2), channel_id=1, replica_groups=mesh['row'=8,'col'=4] {'row'}, dimensions={0}, use_global_device_ids=true | all-gather | bytes 147456 | tf_op jit(solution)/shard_map/all_gather | solution.py:45
  46.7 8.3 %all_gather.21 = bf16[8,4,1024]{2,1,0:T(4,128)(2,1)S(1)} all-gather(bf16[2,4,1024]{2,1,0:T(4,128)(2,1)S(1)} %copy-done.2), channel_id=1, replica_groups=mesh['row'=8,'col'=4] {'col'}, dimensions={0}, use_global_device_ids=true | all-gather | bytes 81920 | tf_op jit(solution)/shard_map/all_gather | solution.py:51
  55.1 14.0 %all_gather.24 = bf16[16,4,1024]{2,1,0:T(4,128)(2,1)S(1)} all-gather(bf16[2,4,1024]{2,1,0:T(4,128)(2,1)S(1)} %copy-done.3), channel_id=1, replica_groups=mesh['row'=8,'col'=4] {'row'}, dimensions={0}, use_global_device_ids=true | all-gather | bytes 147456 | tf_op jit(solution)/shard_map/all_gather | solution.py:44
  69.0 7.3 %all_gather.22 = bf16[8,4,1024]{2,1,0:T(4,128)(2,1)S(1)} all-gather(bf16[2,4,1024]{2,1,0:T(4,128)(2,1)S(1)} %copy-done.3), channel_id=1, replica_groups=mesh['row'=8,'col'=4] {'col'}, dimensions={0}, use_global_device_ids=true | all-gather | bytes 81920 | tf_op jit(solution)/shard_map/all_gather | solution.py:50
  77.5 0.6 copy-done.4
  78.1 12.8 %all-gather = bf16[8,2,512]{2,1,0:T(2,128)(2,1)S(1)} all-gather(bf16[1,2,512]{2,1,0:T(2,128)(2,1)S(1)} %bitcast.64), channel_id=1, replica_groups=mesh['row'=8,'col'=4] {'row'}, dimensions={0}, use_global_device_ids=true | all-gather | bytes 18432 | tf_op jit(solution)/shard_map/all_gather | solution.py:46
  90.9 33.2 %while.14 = (s32[]{:T(128)}, f32[8,16,32]{2,1,0:T(8,128)S(1)}, bf16[8,16,1024]{2,1,0:T(8,128)(2,1)S(1)}, bf16[16,16,1024]{2,1,0:T(8,128)(2,1)S(1)}, bf16[16,16,3...) while((s32[]{:T(128)}, f32[8,16,32]{2,1,0:T(8,128)S(1)}, ...), condition=%wide.region_3.4_spmd.clone, body=%wide.region_2.3_spmd.clone.sunk | while | flops 14714503 | bytes 2319689 | solution.py:74
  91.0 0.7 constant_dynamic-slice_fusion.2
  91.9 0.6 gather_fusion
  93.0 0.5 copy.39
  93.6 1.1 convolution_bitcast_fusion.8
  95.1 0.7 constant_dynamic-slice_fusion.2
  96.0 0.6 gather_fusion
  97.2 0.5 copy.39
  97.8 1.1 convolution_bitcast_fusion.8
  99.3 0.7 constant_dynamic-slice_fusion.2
  100.2 0.6 gather_fusion
  101.3 0.5 copy.39
  101.9 1.1 convolution_bitcast_fusion.8
  103.4 0.7 constant_dynamic-slice_fusion.2
  104.3 0.6 gather_fusion
  105.5 0.5 copy.39
  106.1 1.1 convolution_bitcast_fusion.8
  107.6 0.7 constant_dynamic-slice_fusion.2
  108.5 0.6 gather_fusion
  109.6 0.5 copy.39
  110.2 1.1 convolution_bitcast_fusion.8
  111.7 0.7 constant_dynamic-slice_fusion.2
  112.6 0.6 gather_fusion
  114.4 1.1 convolution_bitcast_fusion.8
  115.9 0.7 constant_dynamic-slice_fusion.2
  116.8 0.6 gather_fusion
  118.5 1.1 convolution_bitcast_fusion.8
  120.0 0.7 constant_dynamic-slice_fusion.2
  121.0 0.6 gather_fusion
  122.7 1.1 convolution_bitcast_fusion.8
  124.2 0.6 copy-done
  125.4 21.2 %reduce-scatter.4.cloned.1.call-done = f32[1,2,16,32]{3,2,1,0:T(8,128)} async-done(((f32[4,2,16,32]{3,2,1,0:T(8,128)}), f32[1,2,16,32]{3,2,1,0:T(8,128)}) %reduce-scatter.4.cloned.1.call-update) | async-done | bytes 4112
  146.6 44.5 %all-reduce.6.cloned.1.call-done = f32[1024,32]{0,1:T(8,128)} async-done(((f32[1024,32]{0,1:T(8,128)}), f32[1024,32]{0,1:T(8,128)}) %all-reduce.6.cloned.1.call-update) | async-done | bytes 131088 | tf_op jit(solution)/shard_map/psum | solution.py:40
  191.2 1.1 fusion.17
  192.5 39.3 %psum.23 = f32[32,32]{0,1:T(8,128)S(1)} all-reduce(f32[32,32]{0,1:T(8,128)S(1)} %convolution_bitcast_fusion.4), channel_id=1, replica_groups=mesh['row'=8,'col'=4] {'row','col'}, use_global_device_ids=true, to_apply=%region_5.6 | all-reduce | flops 1024 | bytes 8192 | tf_op jit(solution)/shard_map/psum | solution.py:96
  232.0 0.7 reshape.61
  232.7 0.7 copy.24
  (98 shorter events, 12.7 us)
Async XLA Ops:
  8.0 116.9 %all-reduce.4.cloned.1.call-start = ((), (), s32[]{:S(2)}) async-start(), calls=%async_computation.1 | async-start | bytes 262144 | tf_op jit(solution)/shard_map/psum | solution.py:39
  10.5 22.3 %copy-start.2 = (bf16[2,4,1024]{2,1,0:T(4,128)(2,1)S(1)}, bf16[2,4,1024]{2,1,0:T(4,128)(2,1)}, u32[]{:S(2)}) copy-start(bf16[2,4,1024]{2,1,0:T(4,128)(2,1)} %param.12) | copy-start | bytes 49156
  10.5 0.7 copy-start.6
  10.6 136.1 %reduce-scatter.4.cloned.1.call-start = ((), (), s32[]{:S(2)}) async-start(), calls=%async_computation.3 | async-start | bytes 81920
  46.7 8.3 %copy-start.3 = (bf16[2,4,1024]{2,1,0:T(4,128)(2,1)S(1)}, bf16[2,4,1024]{2,1,0:T(4,128)(2,1)}, u32[]{:S(2)}) copy-start(bf16[2,4,1024]{2,1,0:T(4,128)(2,1)} %param.11) | copy-start | bytes 49156
  77.4 0.7 copy-start.4
  124.2 0.6 copy-start
  124.8 66.3 %all-reduce.6.cloned.1.call-start = ((), (), s32[]{:S(2)}) async-start(), calls=%async_computation.2 | async-start | bytes 262144 | tf_op jit(solution)/shard_map/psum | solution.py:40
  124.9 66.2 %copy-start.1 = (bf16[2,16,1024]{2,1,0:T(8,128)(2,1)S(1)}, bf16[2,16,1024]{2,1,0:T(8,128)(2,1)}, u32[]{:S(2)}) copy-start(bf16[2,16,1024]{2,1,0:T(8,128)(2,1)} %param.10) | copy-start | bytes 196612
  124.9 66.2 %copy-start.5 = (f32[1024]{0:T(1024)S(1)}, f32[1024]{0:T(1024)}, u32[]{:S(2)}) copy-start(f32[1024]{0:T(1024)} %param.13) | copy-start | bytes 12292
  124.9 66.2 %copy-start.7 = (f32[2,16]{1,0:T(2,128)S(1)}, f32[2,16]{1,0:T(2,128)}, u32[]{:S(2)}) copy-start(f32[2,16]{1,0:T(2,128)} %param.15) | copy-start | bytes 388
Sparse Core Ops, SparseCore 0:
  11.1 57.6 all-reduce.3
Sparse Core Ops, SparseCore 1:
  124.9 21.7 reduce-scatter.3
  149.4 41.7 all-reduce.5
